TPU v7x, 32 devices: a whole 2x2x4 slice. The times are simulated.
32 devices in a mesh: emb: 4 (over x, core), heads: 8 (over z, y).
Axes of the slice: x: 2, y: 2, z: 4, core: 2. Of those that a mesh axis runs over, the one named last changes fastest.
Arguments:
- hidden_in: bfloat16 [16, 8192], P(None, 'emb'), may hold values from -6 to 6
- w_z: bfloat16 [8192, 16384], P('emb', 'heads'), may hold values from -0.0625 to 0.0625
- w_x: bfloat16 [8192, 16384], P('emb', 'heads'), may hold values from -0.0625 to 0.0625
- w_bc: bfloat16 [8192, 4096], P('emb'), may hold values from -0.0625 to 0.0625
- w_dt: bfloat16 [8192, 256], P('emb', 'heads'), may hold values from -0.0625 to 0.0625
- dt_bias: float32 [256], P('heads'), may hold values from -4 to -1
- a_log: float32 [256], P('heads'), may hold values from 0 to 2.77
- skip_gain: float32 [256], P('heads'), may hold values from 0.5 to 2
- conv_x: bfloat16 [16, 3, 16384], P('emb', None, 'heads'), may hold values from -6 to 6
- conv_bc: bfloat16 [16, 3, 4096], P('emb'), may hold values from -6 to 6
- conv_wx: float32 [4, 16384], P(None, 'heads'), may hold values from -3 to 3
- conv_wbc: float32 [4, 4096], replicated, may hold values from -3 to 3
- ssm_state: float32 [16, 256, 64, 256], P('emb', 'heads'), may hold values from -0.6 to 0.6
- norm_gain: float32 [16384], P('heads'), may hold values from 0.5 to 1.5
- w_out: bfloat16 [16384, 8192], P('heads', 'emb'), may hold values from -0.046875 to 0.046875
Outputs:
- mixed: bfloat16 [16, 8192], P(None, 'emb')
- new_state: float32 [16, 256, 64, 256], P('emb', 'heads')
All inputs are finite; a program needn't handle non-finite values.
Results may differ from a plain program's by a relative error of at most 0.0051.
Values may be sent and summed in bfloat16 or wider, within the bound.
A program may use at most 128 MiB of HBM per device.

v0:
```python
import jax
import jax.numpy as jnp
from jax import lax
from jax.sharding import PartitionSpec as P

H = 256
P_SIZE = 64
N = 256
G = 8


def from_partner(value, axis, apart):
    mask = 2**apart
    pairs = [(source, source ^ mask) for source in range(lax.axis_size(axis))]
    return lax.ppermute(value, axis, pairs)


def on_device(
    hidden_in,
    w_z,
    w_x,
    w_bc,
    w_dt,
    dt_bias,
    a_log,
    skip_gain,
    conv_x,
    conv_bc,
    conv_wx,
    conv_wbc,
    ssm_state,
    norm_gain,
    w_out,
):
    heads_dev = w_dt.shape[1]
    emb_rows = w_bc.shape[0]
    batch_dev = conv_x.shape[0]
    group_span = lax.axis_size("heads") // G
    my_group = lax.axis_index("heads") // group_span
    bc_cols = lax.dynamic_slice_in_dim(w_bc.reshape(emb_rows, 2, G, N), my_group, 1, 2).reshape(
        emb_rows, 2 * N
    )
    z_part = jnp.dot(hidden_in, w_z, preferred_element_type=jnp.float32)
    x_part = jnp.dot(hidden_in, w_x, preferred_element_type=jnp.float32)
    bc_part = jnp.dot(hidden_in, bc_cols, preferred_element_type=jnp.float32)
    dt_part = jnp.dot(hidden_in, w_dt, preferred_element_type=jnp.float32)
    summed_all = lax.psum((z_part, x_part, bc_part, dt_part), "emb")
    first_row = lax.axis_index("emb") * batch_dev
    z_pre = lax.dynamic_slice_in_dim(summed_all[0], first_row, batch_dev, 0)
    x_pre = lax.dynamic_slice_in_dim(summed_all[1], first_row, batch_dev, 0)
    bc_pre = lax.dynamic_slice_in_dim(summed_all[2], first_row, batch_dev, 0)
    dt_pre = lax.dynamic_slice_in_dim(summed_all[3], first_row, batch_dev, 0)
    window_x = jnp.concatenate([conv_x.astype(jnp.float32), x_pre[:, None, :]], axis=1)
    x_conv = jax.nn.silu(jnp.sum(window_x * conv_wx[None], axis=1))
    taps_prev = conv_bc.shape[1]
    bc_state = lax.dynamic_slice_in_dim(
        conv_bc.reshape(batch_dev, taps_prev, 2, G, N), my_group, 1, 3
    ).reshape(batch_dev, taps_prev, 2 * N)
    bc_taps = lax.dynamic_slice_in_dim(
        conv_wbc.reshape(taps_prev + 1, 2, G, N), my_group, 1, 2
    ).reshape(taps_prev + 1, 2 * N)
    window_bc = jnp.concatenate([bc_state.astype(jnp.float32), bc_pre[:, None, :]], axis=1)
    bc_conv = jax.nn.silu(jnp.sum(window_bc * bc_taps[None], axis=1)).reshape(batch_dev, 2, N)
    b_group = bc_conv[:, 0]
    c_group = bc_conv[:, 1]
    step_size = jax.nn.softplus(dt_pre + dt_bias[None])
    decay_rate = jnp.exp(-jnp.exp(a_log)[None] * step_size)
    x_heads = x_conv.reshape(batch_dev, heads_dev, P_SIZE)
    new_state = (
        decay_rate[:, :, None, None] * ssm_state
        + (step_size[:, :, None] * x_heads)[..., None] * b_group[:, None, None, :]
    )
    readout = jnp.einsum("bhpn,bn->bhp", new_state, c_group, precision=lax.Precision.HIGHEST)
    readout = readout + skip_gain[None, :, None] * x_heads
    gated = readout.reshape(batch_dev, heads_dev * P_SIZE) * jax.nn.silu(z_pre)
    group_total = jnp.sum(gated * gated, axis=-1)
    span_bits = group_span.bit_length() - 1
    for level in range(span_bits):
        partner = from_partner(group_total, "heads", level)
        group_total = group_total + partner
    mean_sq = group_total / (H * P_SIZE // G)
    inv_rms = lax.rsqrt(mean_sq + 1e-05)
    normed = (gated * inv_rms[:, None] * norm_gain[None]).astype(jnp.bfloat16)
    whole_rows = lax.all_gather(normed, "emb", axis=0, tiled=True)
    partial_value = jnp.dot(whole_rows, w_out, preferred_element_type=jnp.float32)
    mixed = lax.psum(partial_value, "heads").astype(jnp.bfloat16)
    return (mixed, new_state)


def solution(mesh):
    in_specs = (
        P(None, "emb"),
        P("emb", "heads"),
        P("emb", "heads"),
        P("emb", None),
        P("emb", "heads"),
        P("heads"),
        P("heads"),
        P("heads"),
        P("emb", None, "heads"),
        P("emb", None, None),
        P(None, "heads"),
        P(),
        P("emb", "heads", None, None),
        P("heads"),
        P("heads", "emb"),
    )
    out_specs = (P(None, "emb"), P("emb", "heads", None, None))
    return jax.shard_map(
        on_device, mesh=mesh, in_specs=in_specs, out_specs=out_specs, check_vma=False
    )
```

profile of v0, /device:TPU:0, one launch (start us, length us, event | category | flops | bytes accessed | tf_op | source)
XLA Modules:
  0.0 130.3 jit_solution(5878489030706171209)
XLA Ops:
  7.2 0.0 all-reduce.5.cloned.1.call-start
  7.2 5.4 %fusion.8 = f32[16,2048]{1,0:T(8,128)} fusion(bf16[16,2048]{1,0:T(8,128)(2,1)} %param.15, bf16[2048,2048]{1,0:T(8,128)(2,1)} %param.17), kind=kOutput, calls=%fused_computation.30 | convolution fusion | flops 134217728 | bytes 8585216 | tf_op jit(solution)/shard_map/dot_general | solution.py:44
  12.7 0.4 copy-done.2
  13.1 1.9 %fusion.9 = f32[16,2048]{1,0:T(8,128)} fusion(bf16[16,2048]{1,0:T(8,128)(2,1)S(1)} %copy-done.3, bf16[2048,2048]{1,0:T(8,128)(2,1)S(1)} %copy-done.2), kind=kOutput, calls=%fused_computation.31 | convolution fusion | flops 134217728 | bytes 8585216 | tf_op jit(solution)/shard_map/dot_general | solution.py:43
  15.1 22.7 %copy.18 = bf16[2048,4096]{0,1:T(8,128)(2,1)} copy(bf16[2048,4096]{1,0:T(8,128)(2,1)} %param.18) | data formatting | bytes 33554432 | tf_op args[3]
  37.7 1.7 %constant_dynamic-slice_fusion = bf16[2048,2,1,256]{0,3,2,1:T(8,128)(2,1)S(1)} fusion(bf16[2048,2,8,256]{0,3,2,1:T(8,128)(2,1)} %bitcast.41, s32[]{:T(128)S(6)} %select_n.20), kind=kLoop, calls=%fused_computation.26 | loop fusion | bytes 4194308 | tf_op jit(solution)/shard_map/dynamic_slice | solution.py:40
  39.5 0.6 convolution_bitcast_fusion
  40.1 0.2 fusion.7
  40.3 0.1 reshape.54
  40.4 0.1 convert_reduce_fusion
  40.6 13.2 %all-reduce = (f32[16,512]{1,0:T(8,128)S(1)}, f32[16,32]{1,0:T(8,128)S(1)}) all-reduce(f32[16,512]{1,0:T(8,128)S(1)} %convolution_bitcast_fusion, f32[16,32]{1,0:T(8,128)S(1)} %fusion.7), channel_id=1, replica_groups=mesh['emb'=4,'heads'=8] {'emb'}, use_global_device_ids=true, to_apply=%region_3.4 | all-reduce | flops 8704 | bytes 69632 | tf_op jit(solution)/shard_map/psum | solution.py:47
  53.9 0.9 dynamic-slice_bitcast_fusion
  54.9 0.1 reduce_sum.32
  55.0 0.1 broadcast_multiply_fusion
  55.0 4.7 %multiply_add_fusion = f32[4,32,64,256]{3,2,1,0:T(8,128)S(1)} fusion(f32[4,32,64,256]{3,2,1,0:T(8,128)} %param.27, f32[4,256]{1,0:T(4,128)S(1)} %get-tuple-element.11, f32[4,32,64]{2,1,0:T(8,128)S(1)} %broadcast_multiply_fusion, f32[4,32]{1,0:T(4,128)S(1)} %get-tuple-element.8), kind=kLoop, calls=%fused_computation | loop fusion | flops 6291456 | bytes 16814592 | tf_op jit(solution)/shard_map/add | solution.py:70
  59.8 3.4 %copy-done.1 = f32[4,32,64,256]{3,2,1,0:T(8,128)} copy-done((f32[4,32,64,256]{3,2,1,0:T(8,128)}, f32[4,32,64,256]{3,2,1,0:T(8,128)S(1)}, u32[]{:S(2)}) %copy-start.1) | copy-done | bytes 8388632
  63.2 9.8 %fusion.4 = f32[4,1,32,64]{3,1,2,0:T(1,128)S(1)} fusion(f32[4,32,64,256]{3,2,1,0:T(8,128)S(1)} %multiply_add_fusion, f32[4,256,1,1]{1,0,2,3:T(4,128)S(1)} %get-tuple-element.10), kind=kOutput, calls=%fused_computation.23 | convolution fusion | flops 25165824 | bytes 8425472 | tf_op jit(solution)/shard_map/bhpn,bn->bhp/dot_general | solution.py:73
  73.0 0.1 multiply_add_fusion.1
  73.1 0.1 reshape.58
  73.2 1.0 multiply_reduce_fusion
  74.2 0.1 fusion.3
  74.3 5.2 %all-gather = bf16[4,4,2048]{2,1,0:T(4,128)(2,1)S(1)} all-gather(bf16[1,4,2048]{2,1,0:T(4,128)(2,1)S(1)} %fusion.3), channel_id=1, replica_groups=mesh['emb'=4,'heads'=8] {'emb'}, dimensions={0}, use_global_device_ids=true | all-gather | bytes 81920 | tf_op jit(solution)/shard_map/all_gather | solution.py:84
  79.6 4.6 %fusion.10 = f32[16,2048]{1,0:T(8,128)S(1)} fusion(bf16[16,2048]{1,0:T(8,128)(2,1)S(1)} %reshape.61, bf16[2048,2048]{1,0:T(8,128)(2,1)} %param.29), kind=kOutput, calls=%fused_computation.32 | convolution fusion | flops 134217728 | bytes 8585216 | tf_op jit(solution)/shard_map/dot_general | solution.py:85
  84.1 39.3 %all-reduce.6 = bf16[16,2048]{1,0:T(8,128)(2,1)} all-reduce(f32[16,2048]{1,0:T(8,128)S(1)} %fusion.10), channel_id=1, replica_groups=mesh['emb'=4,'heads'=8] {'heads'}, use_global_device_ids=true, to_apply=%region_7.8 | all-reduce | flops 32768 | bytes 196608 | tf_op jit(solution)/shard_map/psum | solution.py:86
  (38 shorter events, 0.4 us)
Async XLA Ops:
  7.2 33.0 %copy-start = (bf16[2048,32]{0,1:T(8,128)(2,1)S(1)}, bf16[2048,32]{0,1:T(8,128)(2,1)}, u32[]{:S(2)}) copy-start(bf16[2048,32]{0,1:T(8,128)(2,1)} %param.19) | copy-start | bytes 393220
  7.2 5.5 %copy-start.3 = (bf16[16,2048]{1,0:T(8,128)(2,1)S(1)}, bf16[16,2048]{1,0:T(8,128)(2,1)}, u32[]{:S(2)}) copy-start(bf16[16,2048]{1,0:T(8,128)(2,1)} %param.15) | copy-start | bytes 196612
  7.2 46.7 %all-reduce.5.cloned.1.call-start = ((), (), s32[]{:S(2)}) async-start(), calls=%async_computation | async-start | bytes 524288 | tf_op jit(solution)/shard_map/psum | solution.py:47
  7.2 5.9 %copy-start.2 = (bf16[2048,2048]{1,0:T(8,128)(2,1)S(1)}, bf16[2048,2048]{1,0:T(8,128)(2,1)}, u32[]{:S(2)}) copy-start(bf16[2048,2048]{1,0:T(8,128)(2,1)} %param.16) | copy-start | bytes 25165828
  15.0 25.3 %copy-start.4 = (bf16[4,3,4096]{2,0,1:T(4,128)(2,1)S(1)}, bf16[4,3,4096]{2,0,1:T(4,128)(2,1)}, u32[]{:S(2)}) copy-start(bf16[4,3,4096]{2,0,1:T(4,128)(2,1)} %param.24) | copy-start | bytes 294916
  15.0 25.5 %copy-start.5 = (f32[4,4096]{1,0:T(4,128)S(1)}, f32[4,4096]{1,0:T(4,128)}, u32[]{:S(2)}) copy-start(f32[4,4096]{1,0:T(4,128)} %param.26) | copy-start | bytes 196612
  15.0 38.8 %copy-start.11 = (f32[32]{0:T(128)S(1)}, f32[32]{0:T(128)}, u32[]{:S(2)}) copy-start(f32[32]{0:T(128)} %param.21) | copy-start | bytes 388
  15.0 38.8 %copy-start.6 = (bf16[4,3,2048]{2,0,1:T(4,128)(2,1)S(1)}, bf16[4,3,2048]{2,0,1:T(4,128)(2,1)}, u32[]{:S(2)}) copy-start(bf16[4,3,2048]{2,0,1:T(4,128)(2,1)} %param.23) | copy-start | bytes 147460
  15.0 38.8 %copy-start.10 = (f32[32]{0:T(128)S(1)}, f32[32]{0:T(128)}, u32[]{:S(2)}) copy-start(f32[32]{0:T(128)} %param.20) | copy-start | bytes 388
  15.1 39.7 %copy-start.7 = (f32[4,2048]{1,0:T(4,128)S(1)}, f32[4,2048]{1,0:T(4,128)}, u32[]{:S(2)}) copy-start(f32[4,2048]{1,0:T(4,128)} %param.25) | copy-start | bytes 98308
  59.8 3.4 %copy-start.1 = (f32[4,32,64,256]{3,2,1,0:T(8,128)}, f32[4,32,64,256]{3,2,1,0:T(8,128)S(1)}, u32[]{:S(2)}) copy-start(f32[4,32,64,256]{3,2,1,0:T(8,128)S(1)} %multiply_add_fusion) | copy-start | bytes 25165828
  59.8 13.2 %copy-start.9 = (f32[32]{0:T(128)S(1)}, f32[32]{0:T(128)}, u32[]{:S(2)}) copy-start(f32[32]{0:T(128)} %param.22) | copy-start | bytes 388
  59.8 14.4 %copy-start.8 = (f32[2048]{0:T(1024)S(1)}, f32[2048]{0:T(1024)}, u32[]{:S(2)}) copy-start(f32[2048]{0:T(1024)} %param.28) | copy-start | bytes 24580
Sparse Core Ops, SparseCore 0:
  15.1 35.0 all-reduce.4
where the time goes:
time: 131 us; the launch traced here: 130 us
  blocking collectives  57.7 us (44%)
  local copies, waits for them, and re-layouts  29.5 us (23%)
  matrix products  22.5 us (17%)
  between operations  14.3 us (11%)
  other arithmetic  6.23 us (5%)
    psum x1, blocking collectives, on_device(): mixed = lax.psum(partial_value, 'heads').astype(jnp.bfloat16)  39.3 us
    unnamed x28, local copies, waits for them, and re-layouts  26.6 us
    psum x1, blocking collectives, on_device(): summed_all = lax.psum((z_part, x_part, bc_part, dt_part), 'emb')  13.2 us
    dot_general x1, matrix products, on_device(): jnp.einsum('bhpn,bn->bhp', new_state, c_group, precision=lax.Precision.HI...  9.83 us
    dot_general x1, matrix products, on_device(): x_part = jnp.dot(hidden_in, w_x, preferred_element_type=jnp.float32)  5.43 us
    all_gather x1, blocking collectives, on_device(): whole_rows = lax.all_gather(normed, 'emb', axis=0, tiled=True)  5.23 us
    add x1, other arithmetic, on_device(): decay_rate[:, :, None, None] * ssm_state  4.75 us
    dot_general x1, matrix products, on_device(): jnp.dot(whole_rows, w_out, preferred_element_type=jnp.float32)  4.58 us
  transfers between devices with their start and end apart: 1, of which 0 were waited for; matrix products, arithmetic and copies ran while one was open for 20% of the time, Pallas kernels for 0%

commit v1 on v0

--- a/solution.py
+++ b/solution.py
@@ -83,7 +83,7 @@
     normed = (gated * inv_rms[:, None] * norm_gain[None]).astype(jnp.bfloat16)
     whole_rows = lax.all_gather(normed, "emb", axis=0, tiled=True)
     partial_value = jnp.dot(whole_rows, w_out, preferred_element_type=jnp.float32)
-    mixed = lax.psum(partial_value, "heads").astype(jnp.bfloat16)
+    mixed = jnp.sum(lax.all_gather(partial_value, "heads"), axis=0).astype(jnp.bfloat16)
     return (mixed, new_state)
 
 

time: 131 us -> 136 us (1.038)
  waiting for transfers between devices: 0.04 us -> 41.2 us
  blocking collectives: 57.7 us -> 18.4 us
  other arithmetic: 6.23 us -> 8.15 us
    all_gather x0 -> x1, waiting for transfers between devices: none -> 41.1 us  [on_device(): lax.all_gather(partial_value, 'heads')]
    psum x1 -> x0, blocking collectives: 39.3 us -> none  [on_device(): mixed = lax.psum(partial_value, 'heads').astype(jnp.bfloat16)]
    reduce_sum x0 -> x1, other arithmetic: none -> 1.92 us  [on_device(): jnp.sum(lax.all_gather(partial_value, 'heads'), axis=0).astype(jnp.bfloat16)]
  transfers between devices with their start and end apart: 1 -> 2, of which waited for: 0 -> 1; matrix products, arithmetic and copies ran while one was open for 20% -> 19% of each run, Pallas kernels for 0% -> 0%
where the time goes in v1:
time: 136 us; the launch traced here: 135 us
  waiting for transfers between devices  41.2 us (30%)
  local copies, waits for them, and re-layouts  29.5 us (22%)
  matrix products  23.1 us (17%)
  blocking collectives  18.4 us (14%)
  between operations  14.3 us (11%)
  other arithmetic  8.15 us (6%)
    all_gather x1, waiting for transfers between devices, on_device(): lax.all_gather(partial_value, 'heads')  41.1 us
    unnamed x28, local copies, waits for them, and re-layouts  26.5 us
    psum x1, blocking collectives, on_device(): summed_all = lax.psum((z_part, x_part, bc_part, dt_part), 'emb')  13.2 us
    dot_general x1, matrix products, on_device(): jnp.einsum('bhpn,bn->bhp', new_state, c_group, precision=lax.Precision.HI...  9.83 us
    dot_general x1, matrix products, on_device(): x_part = jnp.dot(hidden_in, w_x, preferred_element_type=jnp.float32)  5.43 us
    all_gather x1, blocking collectives, on_device(): whole_rows = lax.all_gather(normed, 'emb', axis=0, tiled=True)  5.23 us
    dot_general x1, matrix products, on_device(): jnp.dot(whole_rows, w_out, preferred_element_type=jnp.float32)  5.23 us
    add x1, other arithmetic, on_device(): decay_rate[:, :, None, None] * ssm_state  4.75 us
  transfers between devices with their start and end apart: 2, of which 1 were waited for; matrix products, arithmetic and copies ran while one was open for 19% of the time, Pallas kernels for 0%

profile of v1, /device:TPU:0, one launch (start us, length us, event | category | flops | bytes accessed | tf_op | source)
XLA Modules:
  0.0 134.8 jit_solution(4964939909078449814)
XLA Ops:
  7.2 5.4 %fusion.8 = f32[16,2048]{1,0:T(8,128)} fusion(bf16[16,2048]{1,0:T(8,128)(2,1)} %param.15, bf16[2048,2048]{1,0:T(8,128)(2,1)} %param.17), kind=kOutput, calls=%fused_computation.30 | convolution fusion | flops 134217728 | bytes 8585216 | tf_op jit(solution)/shard_map/dot_general | solution.py:44
  12.7 0.4 copy-done.2
  13.1 1.9 %fusion.9 = f32[16,2048]{1,0:T(8,128)} fusion(bf16[16,2048]{1,0:T(8,128)(2,1)S(1)} %copy-done.3, bf16[2048,2048]{1,0:T(8,128)(2,1)S(1)} %copy-done.2), kind=kOutput, calls=%fused_computation.31 | convolution fusion | flops 134217728 | bytes 8585216 | tf_op jit(solution)/shard_map/dot_general | solution.py:43
  15.1 22.6 %copy.18 = bf16[2048,4096]{0,1:T(8,128)(2,1)} copy(bf16[2048,4096]{1,0:T(8,128)(2,1)} %param.18) | data formatting | bytes 33554432 | tf_op args[3]
  37.7 1.7 %constant_dynamic-slice_fusion = bf16[2048,2,1,256]{0,3,2,1:T(8,128)(2,1)S(1)} fusion(bf16[2048,2,8,256]{0,3,2,1:T(8,128)(2,1)} %bitcast.42, s32[]{:T(128)S(6)} %select_n.20), kind=kLoop, calls=%fused_computation.26 | loop fusion | bytes 4194308 | tf_op jit(solution)/shard_map/dynamic_slice | solution.py:40
  39.5 0.6 convolution_bitcast_fusion
  40.1 0.2 fusion.7
  40.3 0.1 reshape.54
  40.4 0.1 convert_reduce_fusion
  40.6 13.2 %all-reduce = (f32[16,512]{1,0:T(8,128)S(1)}, f32[16,32]{1,0:T(8,128)S(1)}) all-reduce(f32[16,512]{1,0:T(8,128)S(1)} %convolution_bitcast_fusion, f32[16,32]{1,0:T(8,128)S(1)} %fusion.7), channel_id=1, replica_groups=mesh['emb'=4,'heads'=8] {'emb'}, use_global_device_ids=true, to_apply=%region_3.4 | all-reduce | flops 8704 | bytes 69632 | tf_op jit(solution)/shard_map/psum | solution.py:47
  54.0 0.9 dynamic-slice_bitcast_fusion
  54.9 0.1 reduce_sum.41
  55.0 0.1 broadcast_multiply_fusion
  55.1 4.7 %multiply_add_fusion = f32[4,32,64,256]{3,2,1,0:T(8,128)S(1)} fusion(f32[4,32,64,256]{3,2,1,0:T(8,128)} %param.27, f32[4,256]{1,0:T(4,128)S(1)} %get-tuple-element.11, f32[4,32,64]{2,1,0:T(8,128)S(1)} %broadcast_multiply_fusion, f32[4,32]{1,0:T(4,128)S(1)} %get-tuple-element.8), kind=kLoop, calls=%fused_computation | loop fusion | flops 6291456 | bytes 16814592 | tf_op jit(solution)/shard_map/add | solution.py:70
  59.9 3.4 %copy-done.1 = f32[4,32,64,256]{3,2,1,0:T(8,128)} copy-done((f32[4,32,64,256]{3,2,1,0:T(8,128)}, f32[4,32,64,256]{3,2,1,0:T(8,128)S(1)}, u32[]{:S(2)}) %copy-start.1) | copy-done | bytes 8388632
  63.2 9.8 %fusion.4 = f32[4,1,32,64]{3,1,2,0:T(1,128)S(1)} fusion(f32[4,32,64,256]{3,2,1,0:T(8,128)S(1)} %multiply_add_fusion, f32[4,256,1,1]{1,0,2,3:T(4,128)S(1)} %get-tuple-element.10), kind=kOutput, calls=%fused_computation.23 | convolution fusion | flops 25165824 | bytes 8425472 | tf_op jit(solution)/shard_map/bhpn,bn->bhp/dot_general | solution.py:73
  73.1 0.1 multiply_add_fusion.1
  73.2 0.1 reshape.58
  73.3 1.0 multiply_reduce_fusion
  74.3 0.1 fusion.3
  74.3 5.2 %all-gather.1 = bf16[4,4,2048]{2,1,0:T(4,128)(2,1)S(1)} all-gather(bf16[1,4,2048]{2,1,0:T(4,128)(2,1)S(1)} %fusion.3), channel_id=1, replica_groups=mesh['emb'=4,'heads'=8] {'emb'}, dimensions={0}, use_global_device_ids=true | all-gather | bytes 81920 | tf_op jit(solution)/shard_map/all_gather | solution.py:84
  79.6 5.2 %fusion.10 = f32[16,2048]{1,0:T(8,128)} fusion(bf16[16,2048]{1,0:T(8,128)(2,1)S(1)} %reshape.62, bf16[2048,2048]{1,0:T(8,128)(2,1)} %param.29), kind=kOutput, calls=%fused_computation.32 | convolution fusion | flops 134217728 | bytes 8585216 | tf_op jit(solution)/shard_map/dot_general | solution.py:85
  84.9 41.1 %all-gather.4.cloned.1.call-done = f32[128,2048]{1,0:T(8,128)} async-done(((f32[16,2048]{1,0:T(8,128)}), f32[128,2048]{1,0:T(8,128)}) %all-gather.4.cloned.1.call-update) | async-done | bytes 1048592 | tf_op jit(solution)/shard_map/all_gather | solution.py:86
  126.0 1.9 %reduce_sum.45 = bf16[16,2048]{1,0:T(8,128)(2,1)} reduce(f32[8,16,2048]{2,1,0:T(8,128)} %bitcast.44, f32[]{:T(128)} %constant.36.clone.1), dimensions={0}, to_apply=%region_7.8 | reduce | flops 229376 | bytes 1114116 | tf_op jit(solution)/shard_map/reduce_sum | solution.py:86
  (41 shorter events, 0.5 us)
Async XLA Ops:
  7.2 33.0 %copy-start = (bf16[2048,32]{0,1:T(8,128)(2,1)S(1)}, bf16[2048,32]{0,1:T(8,128)(2,1)}, u32[]{:S(2)}) copy-start(bf16[2048,32]{0,1:T(8,128)(2,1)} %param.19) | copy-start | bytes 393220
  7.2 5.5 %copy-start.3 = (bf16[16,2048]{1,0:T(8,128)(2,1)S(1)}, bf16[16,2048]{1,0:T(8,128)(2,1)}, u32[]{:S(2)}) copy-start(bf16[16,2048]{1,0:T(8,128)(2,1)} %param.15) | copy-start | bytes 196612
  7.2 46.8 %all-reduce.4.cloned.1.call-start = ((), (), s32[]{:S(2)}) async-start(), calls=%async_computation.1 | async-start | bytes 524288 | tf_op jit(solution)/shard_map/psum | solution.py:47
  7.2 5.9 %copy-start.2 = (bf16[2048,2048]{1,0:T(8,128)(2,1)S(1)}, bf16[2048,2048]{1,0:T(8,128)(2,1)}, u32[]{:S(2)}) copy-start(bf16[2048,2048]{1,0:T(8,128)(2,1)} %param.16) | copy-start | bytes 25165828
  15.0 111.0 %all-gather.4.cloned.1.call-start = ((), (), s32[]{:S(2)}) async-start(), calls=%async_computation | async-start | bytes 1179648 | tf_op jit(solution)/shard_map/all_gather | solution.py:86
  15.0 25.3 %copy-start.4 = (bf16[4,3,4096]{2,0,1:T(4,128)(2,1)S(1)}, bf16[4,3,4096]{2,0,1:T(4,128)(2,1)}, u32[]{:S(2)}) copy-start(bf16[4,3,4096]{2,0,1:T(4,128)(2,1)} %param.24) | copy-start | bytes 294916
  15.1 25.4 %copy-start.5 = (f32[4,4096]{1,0:T(4,128)S(1)}, f32[4,4096]{1,0:T(4,128)}, u32[]{:S(2)}) copy-start(f32[4,4096]{1,0:T(4,128)} %param.26) | copy-start | bytes 196612
  15.1 38.8 %copy-start.11 = (f32[32]{0:T(128)S(1)}, f32[32]{0:T(128)}, u32[]{:S(2)}) copy-start(f32[32]{0:T(128)} %param.21) | copy-start | bytes 388
  15.1 38.8 %copy-start.6 = (bf16[4,3,2048]{2,0,1:T(4,128)(2,1)S(1)}, bf16[4,3,2048]{2,0,1:T(4,128)(2,1)}, u32[]{:S(2)}) copy-start(bf16[4,3,2048]{2,0,1:T(4,128)(2,1)} %param.23) | copy-start | bytes 147460
  15.1 38.8 %copy-start.10 = (f32[32]{0:T(128)S(1)}, f32[32]{0:T(128)}, u32[]{:S(2)}) copy-start(f32[32]{0:T(128)} %param.20) | copy-start | bytes 388
  15.1 39.7 %copy-start.7 = (f32[4,2048]{1,0:T(4,128)S(1)}, f32[4,2048]{1,0:T(4,128)}, u32[]{:S(2)}) copy-start(f32[4,2048]{1,0:T(4,128)} %param.25) | copy-start | bytes 98308
  59.8 3.4 %copy-start.1 = (f32[4,32,64,256]{3,2,1,0:T(8,128)}, f32[4,32,64,256]{3,2,1,0:T(8,128)S(1)}, u32[]{:S(2)}) copy-start(f32[4,32,64,256]{3,2,1,0:T(8,128)S(1)} %multiply_add_fusion) | copy-start | bytes 25165828
  59.9 13.2 %copy-start.9 = (f32[32]{0:T(128)S(1)}, f32[32]{0:T(128)}, u32[]{:S(2)}) copy-start(f32[32]{0:T(128)} %param.22) | copy-start | bytes 388
  59.9 14.4 %copy-start.8 = (f32[2048]{0:T(1024)S(1)}, f32[2048]{0:T(1024)}, u32[]{:S(2)}) copy-start(f32[2048]{0:T(1024)} %param.28) | copy-start | bytes 24580
Sparse Core Ops, SparseCore 0:
  15.1 35.0 all-reduce.3
  85.0 40.9 all-gather.3
